TPU v7x, 128 devices: a whole 4x4x4 slice. The times are simulated.
128 devices in a mesh: dp: 16 (over x_lo, y, core), layer: 8 (over x_hi, z).
Axes of the slice: x: 4 (x_hi: 2, x_lo: 2; x = x_hi * 2 + x_lo), y: 4, z: 4, core: 2. Of those that a mesh axis runs over, the one named last changes fastest.
Arguments:
- activations: bfloat16 [4096, 8, 7168], P('dp', 'layer'), may hold values from -200 to 200
- labels: int32 [4096], P('dp'), may hold values from 0 to 511
- weights: float32 [7168, 8, 512], P('dp', 'layer'), may hold values from -0.0625 to 0.0625
- first_moment: float32 [7168, 8, 512], P('dp', 'layer'), may hold values from -0.00036621094 to 0.00036621094
- second_moment: float32 [7168, 8, 512], P('dp', 'layer'), may hold values from 2.1287373e-12 to 2.1287373e-11
Outputs:
- new_weights: float32 [7168, 8, 512], P('dp', 'layer')
- new_first: float32 [7168, 8, 512], P('dp', 'layer')
- new_second: float32 [7168, 8, 512], P('dp', 'layer')
- loss: float32 [], replicated
All inputs are finite; a program needn't handle non-finite values.
Results may differ from a plain program's by a relative error of at most 0.0014.
Values may be sent and summed in bfloat16 or wider, within the bound.
A program may use at most 128 MiB of HBM per device.

v0:
```python
import functools
import jax
import jax.numpy as jnp
from jax import lax
from jax.sharding import Mesh
from jax.sharding import PartitionSpec as P

STEP = 10
DP = ("dp_0", "dp_1", "dp_2")
LAYER = ("layer_0", "layer_1")
DP_LAYER = ("dp_0", "dp_1", "dp_2", "layer_0", "layer_1")


def one_axis_at_a_time(shard, axes):
    return functools.reduce(lax.psum, axes, shard)


def shards(activations, labels, weights, first_moment, second_moment):
    tok_rows = activations.shape[0]
    local_layers = activations.shape[1]
    tokens = tok_rows * lax.axis_size(DP)
    layers = local_layers * lax.axis_size(LAYER)
    width = weights.shape[2]
    low_weights = weights.astype(jnp.bfloat16)
    block = activations
    logits = jnp.einsum(
        "tlk,klc->ltc",
        block,
        lax.all_gather(low_weights, DP, axis=0, tiled=True),
        preferred_element_type=jnp.float32,
    )
    top = jnp.max(logits, axis=2, keepdims=True)
    exps = jnp.exp(logits - top)
    denom = jnp.sum(exps, axis=2, keepdims=True)
    classes = jnp.arange(width, dtype=jnp.int32)
    onehot = (labels[None, :, None] == classes[None, None, :]).astype(jnp.float32)
    picked = jnp.sum(logits * onehot, axis=2)
    local_loss = jnp.sum(top[:, :, 0] + jnp.log(denom[:, :, 0]) - picked)
    probs = exps / denom
    slope = ((probs - onehot) / tokens).astype(jnp.bfloat16)
    total = one_axis_at_a_time(local_loss, DP_LAYER)
    regrouped = lax.all_to_all(activations, DP, split_axis=2, concat_axis=0, tiled=True)
    block = regrouped
    grad = jnp.einsum(
        "tlk,ltc->klc",
        block,
        lax.all_gather(slope, DP, axis=1, tiled=True),
        preferred_element_type=jnp.float32,
    )
    local_square = jnp.sum(grad * grad)
    square = one_axis_at_a_time(local_square, DP_LAYER)
    loss = total / (tokens * layers)
    factor = jnp.minimum(1.0, 0.25 / jnp.sqrt(square + 1e-12))
    clipped = factor * grad
    new_first = 0.9 * first_moment + 0.1 * clipped
    new_second = 0.999 * second_moment + 0.001 * clipped * clipped
    new_weights = weights - 0.001 * (new_first / (1.0 - 0.9**STEP)) / (
        jnp.sqrt(new_second / (1.0 - 0.999**STEP)) + 1e-08
    )
    return (new_weights, new_first, new_second, loss)


def solution(mesh):
    finer = Mesh(
        mesh.devices.reshape(2, 4, 2, 2, 4), ("dp_0", "dp_1", "dp_2", "layer_0", "layer_1")
    )
    in_specs = (
        P(DP, LAYER, None),
        P(DP),
        P(DP, LAYER, None),
        P(DP, LAYER, None),
        P(DP, LAYER, None),
    )
    out_specs = (P(DP, LAYER, None), P(DP, LAYER, None), P(DP, LAYER, None), P())
    return jax.shard_map(
        shards, mesh=finer, in_specs=in_specs, out_specs=out_specs, check_vma=False
    )
```

profile of v0, /device:TPU:0, one launch (start us, length us, event | category | flops | bytes accessed | tf_op | source)
XLA Modules:
  0.0 261.6 jit_solution(9206150363318013744)
XLA Ops:
  7.2 0.0 all-gather.4.cloned.1.call-start
  7.2 2.0 copy.43
  9.2 0.0 all-gather.4.cloned.1.call-update
  9.2 0.0 copy-start.3
  9.3 0.0 all-gather.6.cloned.1.call-start
  9.3 50.6 %all-gather.4.cloned.1.call-done = bf16[7168,1,512]{2,0,1:T(8,128)(2,1)} async-done(((bf16[448,1,512]{2,0,1:T(8,128)(2,1)}), bf16[7168,1,512]{2,0,1:T(8,128)(2,1)}) %all-gather.4.cloned.1.call-update) | async-done | bytes 7340048 | tf_op jit(solution)/shard_map/all_gather | solution.py:29
  59.9 6.3 %fusion.8 = (f32[256]{0:T(256)S(1)}, f32[256,512]{1,0:T(8,128)S(1)}) fusion(bf16[7168,1,512]{2,0,1:T(8,128)(2,1)} %all-gather.4.cloned.1.call-done, bf16[256,1,7168]{2,0,1:T(8,128)(2,1)} %param.5), kind=kOutput, calls=%fused_computation.18 | convolution fusion | flops 1879179008 | bytes 11535360 | tf_op jit(solution)/shard_map/tlk,klc->ltc/dot_general | solution.py:26
  66.2 0.0 copy-done.3
  66.2 0.3 select_reduce_fusion
  66.5 0.9 multiply_convert_fusion
  67.4 0.0 all-gather.6.cloned.1.call-update
  67.5 16.4 %copy.25 = bf16[256,1,7168]{0,1,2:T(2,128)(2,1)} copy(bf16[256,1,7168]{2,0,1:T(8,128)(2,1)} %param.5) | data formatting | bytes 7340032 | tf_op args[0]
  83.8 0.5 broadcast.32
  84.4 38.4 %reduce.9 = bf16[7168,256]{1,0:T(8,128)(2,1)} reduce(bf16[7168,1,256]{2,1,0:T(2,128)(2,1)} %bitcast.33, bf16[]{:T(256)} %broadcast.32), dimensions={1}, to_apply=%bitcast.23.reduce_sub_computation | reduce | bytes 7340034
  122.8 10.3 %reshape.68 = bf16[16,2,57344]{2,1,0:T(2,128)(2,1)} reshape(bf16[7168,256]{1,0:T(8,128)(2,1)} %reduce.9) | data formatting | bytes 7340032
  133.1 49.6 %all_to_all.15 = bf16[16,2,57344]{2,1,0:T(2,128)(2,1)} all-to-all(bf16[16,2,57344]{2,1,0:T(2,128)(2,1)} %reshape.68), channel_id=1, replica_groups=mesh['dp_0'=2,'dp_1'=4,'dp_2'=2,'layer_0'=2,'layer_1'=4] {'dp_0','dp_1',..., dimensions={0} | all-to-all | bytes 7340032 | tf_op jit(solution)/shard_map/all_to_all | solution.py:42
  182.7 12.0 %reshape.69 = bf16[7168,1,256]{2,1,0:T(2,128)(2,1)} reshape(bf16[16,2,57344]{2,1,0:T(2,128)(2,1)} %all_to_all.15) | data formatting | bytes 7340032
  194.7 3.7 %copy.32 = bf16[256,1,7168]{0,2,1:T(8,128)(2,1)S(1)} copy(bf16[256,1,7168]{0,1,2:T(2,128)(2,1)} %bitcast.34) | data formatting | bytes 7340032
  198.4 2.3 copy.33
  200.7 0.6 subtract_reduce_fusion
  201.3 0.0 all-gather.6.cloned.1.call-done
  201.3 0.0 copy-start
  201.3 0.0 copy-start.1
  201.3 0.0 copy-start.2
  201.3 7.0 %multiply_reduce_fusion = (f32[]{:T(128)}, f32[512,448]{0,1:T(8,128)}) fusion(bf16[4096,448]{0,1:T(8,128)(2,1)} %bitcast.36, bf16[4096,512]{1,0:T(8,128)(2,1)} %all-gather.6.cloned.1.call-done), kind=kOutput, calls=%fused_computation.10 | convolution fusion | flops 1879506944 | bytes 8781828 | tf_op jit(solution)/shard_map/tlk,ltc->klc/dot_general | solution.py:44
  208.3 5.5 %all-reduce.4 = (f32[]{:T(128)}, f32[]{:T(128)}) all-reduce(f32[]{:T(128)} %get-tuple-element.33, f32[]{:T(128)} %subtract_reduce_fusion), channel_id=1, replica_groups=mesh['dp_0'=2,'dp_1'=4,'dp_2'=2,'layer_0'=2,'layer_1'=4] {'dp_0'}, use_global_device_ids=true, to_apply=%region_3.0 | all-reduce | flops 2 | bytes 16 | tf_op jit(solution)/shard_map/psum | solution.py:15
  213.9 9.2 %all-reduce.1 = (f32[]{:T(128)}, f32[]{:T(128)}) all-reduce(f32[]{:T(128)} %get-tuple-element.26, f32[]{:T(128)} %get-tuple-element.27), channel_id=1, replica_groups=mesh['dp_0'=2,'dp_1'=4,'dp_2'=2,'layer_0'=2,'layer_1'=4] {'dp_1'}, use_global_device_ids=true, to_apply=%region_4.0 | all-reduce | flops 2 | bytes 16 | tf_op jit(solution)/shard_map/psum | solution.py:15
  223.1 3.1 %all-reduce.3 = (f32[]{:T(128)}, f32[]{:T(128)}) all-reduce(f32[]{:T(128)} %get-tuple-element.20, f32[]{:T(128)} %get-tuple-element.21), channel_id=1, replica_groups=mesh['dp_0'=2,'dp_1'=4,'dp_2'=2,'layer_0'=2,'layer_1'=4] {'dp_2'}, use_global_device_ids=true, to_apply=%region_5.0 | all-reduce | flops 2 | bytes 16 | tf_op jit(solution)/shard_map/psum | solution.py:15
  226.2 7.0 %all-reduce.2 = (f32[]{:T(128)}, f32[]{:T(128)}) all-reduce(f32[]{:T(128)} %get-tuple-element.24, f32[]{:T(128)} %get-tuple-element.25), channel_id=1, replica_groups=mesh['dp_0'=2,'dp_1'=4,'dp_2'=2,'layer_0'=2,'layer_1'=4] {'layer_0'}, use_global_device_ids=true, to_apply=%region_6.0 | all-reduce | flops 2 | bytes 16 | tf_op jit(solution)/shard_map/psum | solution.py:15
  233.2 11.5 %all-reduce = (f32[]{:T(128)}, f32[]{:T(128)}) all-reduce(f32[]{:T(128)} %get-tuple-element.22, f32[]{:T(128)} %get-tuple-element.23), channel_id=1, replica_groups=mesh['dp_0'=2,'dp_1'=4,'dp_2'=2,'layer_0'=2,'layer_1'=4] {'layer_1'}, use_global_device_ids=true, to_apply=%region_7.0 | all-reduce | flops 2 | bytes 16 | tf_op jit(solution)/shard_map/psum | solution.py:15
  245.5 0.0 copy-done
  245.5 0.0 copy-done.1
  245.5 0.0 copy-done.2
  245.5 1.8 divide_subtract_fusion
  247.3 1.9 copy.29
  249.2 1.9 copy.30
  251.1 1.9 copy.31
Async XLA Ops:
  7.2 52.7 %all-gather.4.cloned.1.call-start = ((), (), s32[]{:S(2)}) async-start(), calls=%async_computation.1 | async-start | bytes 7798784 | tf_op jit(solution)/shard_map/all_gather | solution.py:29
  9.2 57.0 %copy-start.3 = (s32[256]{0:T(256)S(1)}, s32[256]{0:T(256)}, u32[]{:S(2)}) copy-start(s32[256]{0:T(256)} %param.6) | copy-start | bytes 3076
  9.3 192.0 %all-gather.6.cloned.1.call-start = ((), (), s32[]{:S(2)}) async-start(), calls=%async_computation.2 | async-start | bytes 4456448 | tf_op jit(solution)/shard_map/all_gather | solution.py:47
  201.3 44.2 %copy-start = (f32[448,1,512]{2,1,0:T(1,128)S(1)}, f32[448,1,512]{2,1,0:T(1,128)}, u32[]{:S(2)}) copy-start(f32[448,1,512]{2,1,0:T(1,128)} %param.7) | copy-start | bytes 2752516
  201.3 44.2 %copy-start.1 = (f32[448,1,512]{2,1,0:T(1,128)S(1)}, f32[448,1,512]{2,1,0:T(1,128)}, u32[]{:S(2)}) copy-start(f32[448,1,512]{2,1,0:T(1,128)} %param.8) | copy-start | bytes 2752516
  201.3 44.2 %copy-start.2 = (f32[448,1,512]{2,1,0:T(1,128)S(1)}, f32[448,1,512]{2,1,0:T(1,128)}, u32[]{:S(2)}) copy-start(f32[448,1,512]{2,1,0:T(1,128)} %param.9) | copy-start | bytes 2752516
Sparse Core Ops, SparseCore 0:
  10.2 49.5 all-gather.3
  67.6 38.1 all-gather.5
where the time goes:
time: 263 us; the launch traced here: 262 us
  blocking collectives  86.1 us (33%)
  local copies, waits for them, and re-layouts  52.8 us (20%)
  waiting for transfers between devices  50.6 us (19%)
  other arithmetic  42.1 us (16%)
  between operations  16.6 us (6%)
  matrix products  13.3 us (5%)
    unnamed x18, local copies, waits for them, and re-layouts  52.8 us
    all_gather x1, waiting for transfers between devices, shards(): lax.all_gather(low_weights, DP, axis=0, tiled=True)  50.6 us
    all_to_all x1, blocking collectives, shards(): lax.all_to_all(activations, DP, split_axis=2, concat_axis=0, tiled=True)  49.6 us
    unnamed x1, other arithmetic  38.4 us
    psum x5, blocking collectives, one_axis_at_a_time(): return functools.reduce(lax.psum, axes, shard)  36.5 us
    dot_general x1, matrix products, shards(): jnp.einsum('tlk,ltc->klc', block, lax.all_gather(slope, DP, axis=1, tiled...  7.02 us
    dot_general x1, matrix products, shards(): jnp.einsum('tlk,klc->ltc', block, lax.all_gather(low_weights, DP, axis=0,...  6.33 us
  transfers between devices with their start and end apart: 2, of which 1 were waited for; matrix products, arithmetic and copies ran while one was open for 32% of the time, Pallas kernels for 0%

commit v1 on v0

--- a/solution.py
+++ b/solution.py
@@ -39,7 +39,10 @@
     probs = exps / denom
     slope = ((probs - onehot) / tokens).astype(jnp.bfloat16)
     total = one_axis_at_a_time(local_loss, DP_LAYER)
-    regrouped = lax.all_to_all(activations, DP, split_axis=2, concat_axis=0, tiled=True)
+    regrouped = jnp.concatenate(
+        lax.all_to_all(jnp.stack(jnp.split(activations, lax.axis_size(DP), axis=2)), DP, 0, 0),
+        axis=0,
+    )
     block = regrouped
     grad = jnp.einsum(
         "tlk,ltc->klc",

time: 263 us -> 206 us (0.78)
  other arithmetic: 42.1 us -> 3.66 us
  local copies, waits for them, and re-layouts: 52.8 us -> 26 us
  blocking collectives: 86.1 us -> 95.2 us
    unnamed x1 -> x0, other arithmetic: 38.4 us -> none
    unnamed x18 -> x44, local copies, waits for them, and re-layouts: 52.8 us -> 21.7 us
    all_to_all x1, blocking collectives: 49.6 us -> 57.8 us  [shards(): lax.all_to_all(jnp.stack(jnp.split(activations, lax.axis_size(DP), axis=2...]
    split x0 -> x1, local copies, waits for them, and re-layouts: none -> 4.31 us  [shards(): jnp.split(activations, lax.axis_size(DP), axis=2)]
  transfers between devices with their start and end apart: 2 -> 2, of which waited for: 1 -> 1; matrix products, arithmetic and copies ran while one was open for 32% -> 9% of each run, Pallas kernels for 0% -> 0%
where the time goes in v1:
time: 206 us
  blocking collectives  95.2 us (46%)
  waiting for transfers between devices  50.6 us (25%)
  local copies, waits for them, and re-layouts  26 us (13%)
  between operations  16.8 us (8%)
  matrix products  13.4 us (7%)
  other arithmetic  3.66 us (2%)
    all_to_all x1, blocking collectives, shards(): lax.all_to_all(jnp.stack(jnp.split(activations, lax.axis_size(DP), axis=2...  57.8 us
    all_gather x1, waiting for transfers between devices, shards(): lax.all_gather(low_weights, DP, axis=0, tiled=True)  50.6 us
    psum x5, blocking collectives, one_axis_at_a_time(): return functools.reduce(lax.psum, axes, shard)  37.4 us
    unnamed x44, local copies, waits for them, and re-layouts  21.7 us
    dot_general x1, matrix products, shards(): jnp.einsum('tlk,ltc->klc', block, lax.all_gather(slope, DP, axis=1, tiled...  7.02 us
    dot_general x1, matrix products, shards(): jnp.einsum('tlk,klc->ltc', block, lax.all_gather(low_weights, DP, axis=0,...  6.33 us
    split x1, local copies, waits for them, and re-layouts, shards(): jnp.split(activations, lax.axis_size(DP), axis=2)  4.31 us
  transfers between devices with their start and end apart: 2, of which 1 were waited for; matrix products, arithmetic and copies ran while one was open for 9% of the time, Pallas kernels for 0%

profile of v1, /device:TPU:0, one launch (start us, length us, event | category | flops | bytes accessed | tf_op | source)
XLA Modules:
  0.0 205.7 jit_solution(8805954066591334002)
XLA Ops:
  7.2 0.0 all-gather.4.cloned.1.call-start
  7.2 2.0 copy.88
  9.2 0.0 all-gather.4.cloned.1.call-update
  9.2 0.0 copy-start.3
  9.3 0.0 all-gather.6.cloned.1.call-start
  9.3 50.6 %all-gather.4.cloned.1.call-done = bf16[7168,1,512]{2,0,1:T(8,128)(2,1)} async-done(((bf16[448,1,512]{2,0,1:T(8,128)(2,1)}), bf16[7168,1,512]{2,0,1:T(8,128)(2,1)}) %all-gather.4.cloned.1.call-update) | async-done | bytes 7340048 | tf_op jit(solution)/shard_map/all_gather | solution.py:29
  59.9 6.3 %fusion.9 = (f32[256]{0:T(256)S(1)}, f32[256,512]{1,0:T(8,128)S(1)}) fusion(bf16[7168,1,512]{2,0,1:T(8,128)(2,1)} %all-gather.4.cloned.1.call-done, bf16[256,1,7168]{2,0,1:T(8,128)(2,1)} %param.5), kind=kOutput, calls=%fused_computation.35 | convolution fusion | flops 1879179008 | bytes 11535360 | tf_op jit(solution)/shard_map/tlk,klc->ltc/dot_general | solution.py:26
  66.2 0.0 copy-done.3
  66.2 0.3 select_reduce_fusion
  66.5 0.9 multiply_convert_fusion
  67.4 0.0 all-gather.6.cloned.1.call-update
  67.5 4.3 %fusion.8 = (bf16[256,1,448]{2,0,1:T(8,128)(2,1)S(1)}, bf16[256,1,448]{2,0,1:T(8,128)(2,1)S(1)}, bf16[256,1,448]{2,0,1:T(8,128)(2,1)S(1)}, bf16[256,1,448]{2,0,1...) fusion(bf16[256,1,7168]{2,0,1:T(8,128)(2,1)} %param.5), kind=kLoop, calls=%fused_computation.34 | loop fusion | bytes 7340032 | tf_op jit(solution)/shard_map/split | solution.py:43
  71.8 1.8 copy.62
  73.5 1.8 copy.63
  75.3 1.8 copy.64
  77.1 0.8 copy.65
  77.9 0.1 copy.66
  78.0 0.1 copy.67
  78.2 0.1 copy.68
  78.3 0.1 copy.69
  78.5 0.1 copy.70
  78.6 0.1 copy.71
  78.7 0.1 copy.72
  78.9 0.1 copy.73
  79.0 0.1 copy.74
  79.2 0.1 copy.75
  79.3 0.1 copy.76
  79.4 0.1 copy.77
  79.6 1.0 bitcast_dynamic-update-slice_fusion.15
  80.5 1.0 bitcast_dynamic-update-slice_fusion.14
  81.5 1.0 bitcast_dynamic-update-slice_fusion.13
  82.5 1.0 bitcast_dynamic-update-slice_fusion.12
  83.8 57.8 %all_to_all.5 = bf16[16,256,1,448]{1,3,2,0:T(8,128)(2,1)S(1)} all-to-all(bf16[16,256,1,448]{1,3,2,0:T(8,128)(2,1)S(1)} %bitcast_dynamic-update-slice_fusion), channel_id=1, replica_groups=mesh['dp_0'=2,'dp_1'=4,'dp_2'=2,'layer_0'=2,'layer_1'=4] {'dp_0','dp_1',..., dimensions={0} | all-to-all | bytes 7340032 | tf_op jit(solution)/shard_map/all_to_all | solution.py:43
  141.6 2.3 %copy.78 = bf16[56,8,16,256]{3,1,2,0:T(8,128)(2,1)} copy(bf16[56,8,16,256]{3,1,0,2:T(8,128)(2,1)S(1)} %bitcast.59) | data formatting | bytes 7340032
  143.9 0.6 subtract_reduce_fusion
  144.5 7.0 %multiply_reduce_fusion = (f32[]{:T(128)}, f32[512,448]{0,1:T(8,128)}) fusion(bf16[4096,448]{0,1:T(8,128)(2,1)} %bitcast.60, bf16[4096,512]{1,0:T(8,128)(2,1)} %all-gather.6.cloned.1.call-done), kind=kOutput, calls=%fused_computation.10 | convolution fusion | flops 1879506944 | bytes 8781828 | tf_op jit(solution)/shard_map/tlk,ltc->klc/dot_general | solution.py:47
  151.5 5.5 %all-reduce.4 = (f32[]{:T(128)}, f32[]{:T(128)}) all-reduce(f32[]{:T(128)} %get-tuple-element.49, f32[]{:T(128)} %subtract_reduce_fusion), channel_id=1, replica_groups=mesh['dp_0'=2,'dp_1'=4,'dp_2'=2,'layer_0'=2,'layer_1'=4] {'dp_0'}, use_global_device_ids=true, to_apply=%region_3.0 | all-reduce | flops 2 | bytes 16 | tf_op jit(solution)/shard_map/psum | solution.py:15
  157.0 10.4 %all-reduce.1 = (f32[]{:T(128)}, f32[]{:T(128)}) all-reduce(f32[]{:T(128)} %get-tuple-element.26, f32[]{:T(128)} %get-tuple-element.27), channel_id=1, replica_groups=mesh['dp_0'=2,'dp_1'=4,'dp_2'=2,'layer_0'=2,'layer_1'=4] {'dp_1'}, use_global_device_ids=true, to_apply=%region_4.0 | all-reduce | flops 2 | bytes 16 | tf_op jit(solution)/shard_map/psum | solution.py:15
  167.4 3.1 %all-reduce.3 = (f32[]{:T(128)}, f32[]{:T(128)}) all-reduce(f32[]{:T(128)} %get-tuple-element.20, f32[]{:T(128)} %get-tuple-element.21), channel_id=1, replica_groups=mesh['dp_0'=2,'dp_1'=4,'dp_2'=2,'layer_0'=2,'layer_1'=4] {'dp_2'}, use_global_device_ids=true, to_apply=%region_5.0 | all-reduce | flops 2 | bytes 16 | tf_op jit(solution)/shard_map/psum | solution.py:15
  170.5 7.0 %all-reduce.2 = (f32[]{:T(128)}, f32[]{:T(128)}) all-reduce(f32[]{:T(128)} %get-tuple-element.24, f32[]{:T(128)} %get-tuple-element.25), channel_id=1, replica_groups=mesh['dp_0'=2,'dp_1'=4,'dp_2'=2,'layer_0'=2,'layer_1'=4] {'layer_0'}, use_global_device_ids=true, to_apply=%region_6.0 | all-reduce | flops 2 | bytes 16 | tf_op jit(solution)/shard_map/psum | solution.py:15
  177.6 11.4 %all-reduce = (f32[]{:T(128)}, f32[]{:T(128)}) all-reduce(f32[]{:T(128)} %get-tuple-element.22, f32[]{:T(128)} %get-tuple-element.23), channel_id=1, replica_groups=mesh['dp_0'=2,'dp_1'=4,'dp_2'=2,'layer_0'=2,'layer_1'=4] {'layer_1'}, use_global_device_ids=true, to_apply=%region_7.0 | all-reduce | flops 2 | bytes 16 | tf_op jit(solution)/shard_map/psum | solution.py:15
  189.6 0.0 copy-done
  189.6 0.0 copy-done.1
  189.6 0.0 copy-done.2
  189.7 1.8 divide_subtract_fusion
  191.5 1.9 copy.59
  193.3 1.9 copy.60
  195.2 1.9 copy.61
  (16 shorter events, 0.2 us)
Async XLA Ops:
  7.2 52.7 %all-gather.4.cloned.1.call-start = ((), (), s32[]{:S(2)}) async-start(), calls=%async_computation.1 | async-start | bytes 7798784 | tf_op jit(solution)/shard_map/all_gather | solution.py:29
  9.2 57.0 %copy-start.3 = (s32[256]{0:T(256)S(1)}, s32[256]{0:T(256)}, u32[]{:S(2)}) copy-start(s32[256]{0:T(256)} %param.6) | copy-start | bytes 3076
  9.3 135.2 %all-gather.6.cloned.1.call-start = ((), (), s32[]{:S(2)}) async-start(), calls=%async_computation.2 | async-start | bytes 4456448 | tf_op jit(solution)/shard_map/all_gather | solution.py:50
  144.5 45.2 %copy-start = (f32[448,1,512]{2,1,0:T(1,128)S(1)}, f32[448,1,512]{2,1,0:T(1,128)}, u32[]{:S(2)}) copy-start(f32[448,1,512]{2,1,0:T(1,128)} %param.7) | copy-start | bytes 2752516
  144.5 45.2 %copy-start.1 = (f32[448,1,512]{2,1,0:T(1,128)S(1)}, f32[448,1,512]{2,1,0:T(1,128)}, u32[]{:S(2)}) copy-start(f32[448,1,512]{2,1,0:T(1,128)} %param.8) | copy-start | bytes 2752516
  144.5 45.2 %copy-start.2 = (f32[448,1,512]{2,1,0:T(1,128)S(1)}, f32[448,1,512]{2,1,0:T(1,128)}, u32[]{:S(2)}) copy-start(f32[448,1,512]{2,1,0:T(1,128)} %param.9) | copy-start | bytes 2752516
Sparse Core Ops, SparseCore 0:
  10.2 49.5 all-gather.3
  67.6 71.4 all-gather.5
